TPU v7x, 32 devices: a whole 2x2x4 slice. The times are simulated.
32 devices in a mesh: row: 4 (over z), col: 8 (over y, x, core).
Axes of the slice: x: 2, y: 2, z: 4, core: 2. Of those that a mesh axis runs over, the one named last changes fastest.
Arguments:
- tiles: bfloat16 [4, 8, 128, 128, 128], P('row', 'col'), may hold values from -6 to 6
- tile_row: int32 [4, 8, 128], P('row', 'col'), may hold values from 0 to 63, as said below
- tile_col: int32 [4, 8, 128], P('row', 'col'), may hold values from 0 to 31
- tile_count: int32 [4, 8], P('row', 'col'), may hold values from 16 to 128, as said below
- query_ids: int32 [128], replicated, may hold values from 0 to 32767
- damping: float32 [128], replicated, may hold values from 0.006629126 to 0.026516505
Outputs:
- scores: float32 [32768, 128], P(('row', 'col'))
Inputs may be any that keep to these rules, and one draw needn't show every extreme that they name: `tile_count`: some device holds exactly 128 live slots; slots at or past the count hold arbitrary finite values and are ignored. `tile_row`: positions may repeat within a device; such tiles add. For every device and every col index o, the live slots name at most 4 distinct values among o * 8 to o * 8 + 7, and every device reaches 4 for some o. `query_ids`: ids may repeat.
All inputs are finite; a program needn't handle non-finite values.
Results may differ from a plain program's by a relative error of at most 0.003.
Values may be sent and summed in bfloat16 or wider, within the bound.
A program may use at most 128 MiB of HBM per device.

v0:
```python
import jax
import jax.numpy as jnp
from jax import lax
from jax.sharding import PartitionSpec as P

BPD = 8
TERMS = 4
TOUCH = 4


def dense_partial(tile_block, rows, cols, count, xcol, row_blocks):
    picked = xcol[cols]
    prod = jnp.einsum("tab,tbq->taq", tile_block, picked, preferred_element_type=jnp.float32)
    live = (jnp.arange(tile_block.shape[0], dtype=jnp.int32) < count).astype(jnp.float32)
    prod = prod * live[:, None, None]
    return jax.ops.segment_sum(prod, rows, num_segments=row_blocks)


def touched_sum(part, rows, count, n_col):
    row_blocks, tile, width = part.shape
    live = jnp.arange(rows.shape[0], dtype=jnp.int32) < count
    hits = (rows[None, :] == jnp.arange(row_blocks, dtype=jnp.int32)[:, None]) & live[None, :]
    marked = jnp.any(hits, axis=1).reshape(n_col, BPD)
    rank = jnp.cumsum(marked.astype(jnp.int32), axis=1) - 1
    places = jnp.arange(TOUCH, dtype=jnp.int32)
    select = marked[:, None, :] & (rank[:, None, :] == places[None, :, None])
    rounded = part.astype(jnp.bfloat16).reshape(n_col, BPD, tile, width)
    blocks = jnp.einsum(
        "ojb,obtq->ojtq", select.astype(jnp.bfloat16), rounded, preferred_element_type=jnp.float32
    ).astype(jnp.bfloat16)
    local = jnp.arange(BPD, dtype=jnp.int32)
    block_ids = jnp.sum(select.astype(jnp.int32) * (local[None, None, :] + 1), axis=2) - 1
    got_blocks, got_ids = (
        lax.all_to_all(blocks, "col", split_axis=0, concat_axis=0, tiled=True),
        lax.all_to_all(block_ids, "col", split_axis=0, concat_axis=0, tiled=True),
    )
    placing = (got_ids[:, :, None] == local[None, None, :]).astype(jnp.bfloat16)
    return jnp.einsum("sjb,sjtq->btq", placing, got_blocks, preferred_element_type=jnp.float32)


def shards(tiles, tile_row, tile_col, tile_count, query_ids, damping):
    tile_block = tiles[0, 0]
    rows = tile_row[0, 0]
    cols = tile_col[0, 0]
    count = tile_count[0, 0]
    tile = tile_block.shape[1]
    queries = query_ids.shape[0]
    n_row = lax.axis_size("row")
    n_col = lax.axis_size("col")
    col_index = lax.axis_index("col")
    row_blocks = BPD * n_col
    col_blocks = BPD * n_row
    block_ids = jnp.arange(col_blocks, dtype=jnp.int32)
    global_block = (block_ids // BPD * n_col + col_index) * BPD + block_ids % BPD
    node_ids = global_block[:, None] * tile + jnp.arange(tile, dtype=jnp.int32)[None, :]
    xcol = (node_ids[:, :, None] == query_ids[None, None, :]).astype(jnp.bfloat16)
    scores = jnp.zeros((BPD, tile, queries), jnp.float32)
    coef = jnp.ones((queries,), jnp.float32)
    for step in range(TERMS):
        part = dense_partial(tile_block, rows, cols, count, xcol, row_blocks)
        owned = touched_sum(part, rows, count, n_col)
        scores = scores + coef[None, None, :] * owned
        coef = coef * damping
        if step + 1 < TERMS:
            xcol = lax.all_gather(owned.astype(jnp.bfloat16), "row", axis=0, tiled=True)
    return scores.reshape(BPD * tile, queries)


def solution(mesh):
    in_specs = (
        P("row", "col", None, None, None),
        P("row", "col", None),
        P("row", "col", None),
        P("row", "col"),
        P(),
        P(),
    )
    out_specs = P(("row", "col"), None)
    return jax.shard_map(shards, mesh=mesh, in_specs=in_specs, out_specs=out_specs, check_vma=False)
```

profile of v0, /device:TPU:0, one launch (start us, length us, event | category | flops | bytes accessed | tf_op | source)
XLA Modules:
  0.0 412.1 jit_solution(6482299665852013384)
XLA Ops:
  9.1 5.2 %all-to-all-start = ((s32[8,1,4]{2,1,0:T(1,128)}), s32[8,1,4]{2,1,0:T(1,128)S(1)}, u32[]{:S(2)}, u32[]{:S(2)}) async-start(s32[8,1,4]{2,1,0:T(1,128)} %bitcast.28), calls=%async_computation | async-start | bytes 8192 | tf_op jit(solution)/shard_map/all_to_all | solution.py:35
  17.9 9.1 %multiply_bitcast_fusion.3 = f32[128,128,128]{1,2,0:T(8,128)} fusion(f32[128]{0:T(128)S(1)} %get-tuple-element.14, bf16[1,1,128,128,128]{4,3,2,1,0:T(8,128)(2,1)} %param.6, pred[128,128,128]{2,1,0:T(32,128)(4,1)S(1)} %gather_fusion), kind=kOutput, calls=%fused_computation.11 | convolution fusion | flops 541065216 | bytes 14680576 | tf_op jit(solution)/shard_map/tab,tbq->taq/dot_general | solution.py:13
  27.1 9.0 %copy.75 = f32[128,128,128]{2,1,0:T(8,128)} copy(f32[128,128,128]{1,2,0:T(8,128)} %multiply_bitcast_fusion.3) | data formatting | bytes 16777216 | tf_op jit(solution)/shard_map/mul | solution.py:15
  36.1 2.5 broadcast.158.clone.2
  38.5 26.3 %scatter_fusion = f32[64,128,128]{2,1,0:T(8,128)} fusion(f32[64,128,128]{2,1,0:T(8,128)} %broadcast.158.clone.2, s32[128]{0:T(128)S(1)} %bitcast.92, f32[128,128,128]{2,1,0:T(8,128)} %copy.75), kind=kCustom, calls=%fused_computation.4 | custom fusion | flops 2097152 | bytes 25166336 | tf_op jit(solution)/shard_map/scatter-add | solution.py:16
  64.9 2.6 convert_element_type.68
  69.8 4.1 all-to-all-start.1
  74.0 15.3 %all-to-all-done.1 = bf16[8,4,128,128]{3,1,2,0:T(4,128)(2,1)S(1)} async-done(((bf16[8,4,128,128]{3,1,2,0:T(4,128)(2,1)}), bf16[8,4,128,128]{3,1,2,0:T(4,128)(2,1)S(1)}, u32[]{:S(2)}, u32[]{:S(2)}) %all-to-all-start.1) | async-done | bytes 1048608 | tf_op jit(solution)/shard_map/all_to_all | solution.py:34
  91.0 29.4 %all-gather.4.cloned.1.call-done = bf16[32,128,128]{2,0,1:T(8,128)(2,1)} async-done(((bf16[8,128,128]{2,0,1:T(8,128)(2,1)}), bf16[32,128,128]{2,0,1:T(8,128)(2,1)}) %all-gather.4.cloned.1.call-update) | async-done | bytes 1048592 | tf_op jit(solution)/shard_map/all_gather | solution.py:65
  122.0 3.0 gather_fusion.1
  125.0 9.8 %multiply_bitcast_fusion.2 = f32[128,128,128]{1,2,0:T(8,128)} fusion(f32[128]{0:T(128)S(1)} %get-tuple-element.14, bf16[128,128,128]{2,1,0:T(8,128)(2,1)} %gather_fusion.1, bf16[1,1,128,128,128]{4,3,2,1,0:T(8,128)(2,1)} %param.6), kind=kOutput, calls=%fused_computation.10 | convolution fusion | flops 538968064 | bytes 16777728 | tf_op jit(solution)/shard_map/tab,tbq->taq/dot_general | solution.py:13
  134.8 9.0 %copy.80 = f32[128,128,128]{2,1,0:T(8,128)} copy(f32[128,128,128]{1,2,0:T(8,128)} %multiply_bitcast_fusion.2) | data formatting | bytes 16777216 | tf_op jit(solution)/shard_map/mul | solution.py:15
  143.8 2.5 broadcast.158.clone.1
  146.3 26.3 %scatter_fusion.1 = f32[64,128,128]{2,1,0:T(8,128)} fusion(f32[64,128,128]{2,1,0:T(8,128)} %broadcast.158.clone.1, s32[128]{0:T(128)S(1)} %bitcast.93, f32[128,128,128]{2,1,0:T(8,128)} %copy.80), kind=kCustom, calls=%fused_computation.5 | custom fusion | flops 2097152 | bytes 25166336 | tf_op jit(solution)/shard_map/scatter-add | solution.py:16
  172.6 2.6 convert_element_type.71
  176.6 17.9 %all_to_all.29 = bf16[8,4,128,128]{3,1,2,0:T(4,128)(2,1)S(1)} all-to-all(bf16[8,4,128,128]{3,1,2,0:T(4,128)(2,1)S(1)} %fusion.30), channel_id=1, replica_groups=mesh['row'=4,'col'=8] {'col'}, dimensions={0} | all-to-all | bytes 2097152 | tf_op jit(solution)/shard_map/all_to_all | solution.py:34
  196.2 27.9 %all-gather.6.cloned.1.call-done = bf16[32,128,128]{2,0,1:T(8,128)(2,1)} async-done(((bf16[8,128,128]{2,0,1:T(8,128)(2,1)}), bf16[32,128,128]{2,0,1:T(8,128)(2,1)}) %all-gather.6.cloned.1.call-update) | async-done | bytes 1048592 | tf_op jit(solution)/shard_map/all_gather | solution.py:65
  225.7 3.0 gather_fusion.2
  228.8 9.8 %multiply_bitcast_fusion.1 = f32[128,128,128]{1,2,0:T(8,128)} fusion(f32[128]{0:T(128)S(1)} %get-tuple-element.14, bf16[128,128,128]{2,1,0:T(8,128)(2,1)} %gather_fusion.2, bf16[1,1,128,128,128]{4,3,2,1,0:T(8,128)(2,1)} %param.6), kind=kOutput, calls=%fused_computation.9 | convolution fusion | flops 538968064 | bytes 16777728 | tf_op jit(solution)/shard_map/tab,tbq->taq/dot_general | solution.py:13
  238.6 9.0 %copy.85 = f32[128,128,128]{2,1,0:T(8,128)} copy(f32[128,128,128]{1,2,0:T(8,128)} %multiply_bitcast_fusion.1) | data formatting | bytes 16777216 | tf_op jit(solution)/shard_map/mul | solution.py:15
  247.5 2.5 broadcast.158.clone
  250.0 26.3 %scatter_fusion.2 = f32[64,128,128]{2,1,0:T(8,128)} fusion(f32[64,128,128]{2,1,0:T(8,128)} %broadcast.158.clone, s32[128]{0:T(128)S(1)} %bitcast.94, f32[128,128,128]{2,1,0:T(8,128)} %copy.85), kind=kCustom, calls=%fused_computation.6 | custom fusion | flops 2097152 | bytes 25166336 | tf_op jit(solution)/shard_map/scatter-add | solution.py:16
  276.4 2.6 convert_element_type.74
  280.3 17.9 %all_to_all.30 = bf16[8,4,128,128]{3,1,2,0:T(4,128)(2,1)S(1)} all-to-all(bf16[8,4,128,128]{3,1,2,0:T(4,128)(2,1)S(1)} %fusion.33), channel_id=1, replica_groups=mesh['row'=4,'col'=8] {'col'}, dimensions={0} | all-to-all | bytes 2097152 | tf_op jit(solution)/shard_map/all_to_all | solution.py:34
  299.7 28.1 %all-gather.8.cloned.1.call-done = bf16[32,128,128]{2,0,1:T(8,128)(2,1)} async-done(((bf16[8,128,128]{2,0,1:T(8,128)(2,1)}), bf16[32,128,128]{2,0,1:T(8,128)(2,1)}) %all-gather.8.cloned.1.call-update) | async-done | bytes 1048592 | tf_op jit(solution)/shard_map/all_gather | solution.py:65
  329.5 3.0 gather_fusion.3
  332.5 9.8 %multiply_bitcast_fusion = f32[128,128,128]{1,2,0:T(8,128)} fusion(f32[128]{0:T(128)S(1)} %get-tuple-element.14, bf16[128,128,128]{2,1,0:T(8,128)(2,1)} %gather_fusion.3, bf16[1,1,128,128,128]{4,3,2,1,0:T(8,128)(2,1)} %param.6), kind=kOutput, calls=%fused_computation.8 | convolution fusion | flops 538968064 | bytes 16777728 | tf_op jit(solution)/shard_map/tab,tbq->taq/dot_general | solution.py:13
  342.3 9.0 %copy.90 = f32[128,128,128]{2,1,0:T(8,128)} copy(f32[128,128,128]{1,2,0:T(8,128)} %multiply_bitcast_fusion) | data formatting | bytes 16777216 | tf_op jit(solution)/shard_map/mul | solution.py:15
  353.7 26.3 %scatter_fusion.3 = f32[64,128,128]{2,1,0:T(8,128)} fusion(f32[64,128,128]{2,1,0:T(8,128)} %broadcast.158, s32[128]{0:T(128)S(1)} %bitcast.95, f32[128,128,128]{2,1,0:T(8,128)} %copy.90), kind=kCustom, calls=%fused_computation.7 | custom fusion | flops 2097152 | bytes 25166336 | tf_op jit(solution)/shard_map/scatter-add | solution.py:16
  380.1 2.6 convert_element_type.77
  385.1 3.6 all-to-all-start.4
  388.6 15.3 %all-to-all-done.4 = bf16[8,4,128,128]{3,1,2,0:T(4,128)(2,1)S(1)} async-done(((bf16[8,4,128,128]{3,1,2,0:T(4,128)(2,1)}), bf16[8,4,128,128]{3,1,2,0:T(4,128)(2,1)S(1)}, u32[]{:S(2)}, u32[]{:S(2)}) %all-to-all-start.4) | async-done | bytes 1048608 | tf_op jit(solution)/shard_map/all_to_all | solution.py:34
  (41 shorter events, 27.2 us)
Async XLA Ops:
  9.1 60.8 %all-to-all-start = ((s32[8,1,4]{2,1,0:T(1,128)}), s32[8,1,4]{2,1,0:T(1,128)S(1)}, u32[]{:S(2)}, u32[]{:S(2)}) async-start(s32[8,1,4]{2,1,0:T(1,128)} %bitcast.28), calls=%async_computation | async-start | bytes 8192 | tf_op jit(solution)/shard_map/all_to_all | solution.py:35
  36.1 2.5 copy-start
  69.8 19.4 %all-to-all-start.1 = ((bf16[8,4,128,128]{3,1,2,0:T(4,128)(2,1)}), bf16[8,4,128,128]{3,1,2,0:T(4,128)(2,1)S(1)}, u32[]{:S(2)}, u32[]{:S(2)}) async-start(bf16[8,4,128,128]{3,1,2,0:T(4,128)(2,1)} %fusion.27), calls=%async_computation.1 | async-start | bytes 2097152 | tf_op jit(solution)/shard_map/all_to_all | solution.py:34
  73.9 46.5 %all-gather.4.cloned.1.call-start = ((), (), s32[]{:S(2)}) async-start(), calls=%async_computation.5 | async-start | bytes 1310720 | tf_op jit(solution)/shard_map/all_gather | solution.py:65
  90.8 133.3 %all-gather.6.cloned.1.call-start = ((), (), s32[]{:S(2)}) async-start(), calls=%async_computation.6 | async-start | bytes 1310720 | tf_op jit(solution)/shard_map/all_gather | solution.py:65
  196.0 131.9 %all-gather.8.cloned.1.call-start = ((), (), s32[]{:S(2)}) async-start(), calls=%async_computation.7 | async-start | bytes 1310720 | tf_op jit(solution)/shard_map/all_gather | solution.py:65
  382.6 6.0 %copy-start.1 = (f32[128]{0:T(128)S(1)}, f32[128]{0:T(128)}, u32[]{:S(2)}) copy-start(f32[128]{0:T(128)} %param.11) | copy-start | bytes 1540
  385.1 18.9 %all-to-all-start.4 = ((bf16[8,4,128,128]{3,1,2,0:T(4,128)(2,1)}), bf16[8,4,128,128]{3,1,2,0:T(4,128)(2,1)S(1)}, u32[]{:S(2)}, u32[]{:S(2)}) async-start(bf16[8,4,128,128]{3,1,2,0:T(4,128)(2,1)} %fusion.36), calls=%async_computation.4 | async-start | bytes 2097152 | tf_op jit(solution)/shard_map/all_to_all | solution.py:34
Sparse Core Ops, SparseCore 0:
  90.9 29.4 all-gather.3
  196.1 27.9 all-gather.5
  299.8 27.9 all-gather.7
where the time goes:
time: 414 us; the launch traced here: 412 us
  other arithmetic  119 us (29%)
  waiting for transfers between devices  116 us (28%)
  local copies, waits for them, and re-layouts  62.4 us (15%)
  matrix products  51.3 us (12%)
  blocking collectives  35.7 us (9%)
  between operations  13.9 us (3%)
  starting transfers between devices  13.3 us (3%)
    scatter-add x4, other arithmetic, dense_partial(): return jax.ops.segment_sum(prod, rows, num_segments=row_blocks)  105 us
    all_gather x3, waiting for transfers between devices, shards(): xcol = lax.all_gather(owned.astype(jnp.bfloat16), 'row', axis=0, tiled=True)  85.4 us
    dot_general x4, matrix products, dense_partial(): jnp.einsum('tab,tbq->taq', tile_block, picked, preferred_element_type=jnp...  38.5 us
    mul x4, local copies, waits for them, and re-layouts, dense_partial(): prod = prod * live[:, None, None]  36 us
    all_to_all x2, blocking collectives, touched_sum(): lax.all_to_all(blocks, 'col', split_axis=0, concat_axis=0, tiled=True)  35.7 us
    all_to_all x2, waiting for transfers between devices, touched_sum(): lax.all_to_all(blocks, 'col', split_axis=0, concat_axis=0, tiled=True)  30.5 us
    gather x4, local copies, waits for them, and re-layouts, dense_partial(): picked = xcol[cols]  10.6 us
    convert_element_type x4, other arithmetic, touched_sum(): rounded = part.astype(jnp.bfloat16).reshape(n_col, BPD, tile, width)  10.2 us
  transfers between devices with their start and end apart: 6, of which 5 were waited for; matrix products, arithmetic and copies ran while one was open for 13% of the time, Pallas kernels for 0%

commit v1 on v0

v1 whole, which is shorter than its diff:
```python
import functools

import jax
import jax.numpy as jnp
from jax import lax
from jax.experimental import pallas as pl
from jax.experimental.pallas import tpu as pltpu
from jax.sharding import PartitionSpec as P

BPD = 8
TERMS = 4
TOUCH = 4
HALVES = 2
UNROLL = 8
MESH = pl.DeviceIdType.MESH


def plan(rows, cols, count, n_col, me_col):
    slots = rows.shape[0]
    row_blocks = BPD * n_col
    slot = jnp.arange(slots, dtype=jnp.int32)
    key = jnp.where(slot < count, rows, row_blocks)
    before = (key[None, :] < key[:, None]) | ((key[None, :] == key[:, None]) & (slot[None, :] < slot[:, None]))
    rank = jnp.sum(before.astype(jnp.int32), axis=1)
    at = (rank[None, :] == slot[:, None]).astype(jnp.int32)
    perm = jnp.sum(at * slot[None, :], axis=1)
    scol = jnp.sum(at * cols[None, :], axis=1)
    same = (key[None, :] == key[:, None]) & (slot[None, :] < slot[:, None])
    cont_of = jnp.any(same, axis=1).astype(jnp.int32)
    cont = jnp.sum(at * cont_of[None, :], axis=1)
    blocks = jnp.arange(row_blocks, dtype=jnp.int32)
    hits = key[None, :] == blocks[:, None]
    marked = jnp.any(hits, axis=1).reshape(n_col, BPD)
    last = (jnp.sum((key[None, :] <= blocks[:, None]).astype(jnp.int32), axis=1) - 1).reshape(n_col, BPD)
    local = jnp.arange(BPD, dtype=jnp.int32)
    earlier = marked[:, None, :] & (local[None, None, :] < local[None, :, None])
    place = jnp.sum(earlier.astype(jnp.int32), axis=2)
    places = jnp.arange(TOUCH, dtype=jnp.int32)
    select = marked[:, None, :] & (place[:, None, :] == places[None, :, None])
    ends = jnp.sum(select.astype(jnp.int32) * last[:, None, :], axis=2).reshape(n_col * TOUCH)
    pos = jnp.where(marked, me_col * TOUCH + place, n_col * TOUCH)
    pos = jnp.pad(pos, ((0, 0), (0, 128 - BPD))).reshape(n_col, 1, 128)
    return perm, scol, cont, ends, pos


def katz_kernel(
    n_row, n_col,
    perm, scol, cont, ends,
    pos_ref, qid_ref, damp_ref, tiles_hbm,
    out_ref,
    tiles, run, send, got, xbuf, total, coef, posbuf, pos_smem,
    tile_sem, pos_send, pos_recv, local_sem, send_sem, recv_sem, xsend_sem, xrecv_sem,
):
    me_r = lax.axis_index("row")
    me_c = lax.axis_index("col")
    slots, tile, _ = tiles.shape
    queries = qid_ref.shape[1]
    width = queries // HALVES

    load = pltpu.make_async_copy(tiles_hbm, tiles, tile_sem)
    load.start()
    barrier = pltpu.get_barrier_semaphore()
    for d in range(1, n_col):
        pl.semaphore_signal(barrier, inc=1, device_id=(me_r, lax.rem(me_c + d, n_col)), device_id_type=MESH)
    for d in range(1, n_row):
        pl.semaphore_signal(barrier, inc=1, device_id=(lax.rem(me_r + d, n_row), me_c), device_id_type=MESH)

    lane = lax.broadcasted_iota(jnp.int32, (queries, tile), 1)
    qid = jnp.transpose(jnp.broadcast_to(qid_ref[...], (tile, queries))) - lane
    coef[...] = jnp.transpose(jnp.broadcast_to(damp_ref[...], (tile, queries)))

    def first_x(j, carry):
        base = ((j // BPD * n_col + me_c) * BPD + lax.rem(j, BPD)) * tile
        hot = jnp.where(qid == base, 1.0, 0.0).astype(jnp.bfloat16)
        for h in range(HALVES):
            xbuf[h][j] = hot[h * width:(h + 1) * width]
        return carry

    lax.fori_loop(0, n_row * BPD, first_x, 0)
    for t in range(TERMS * HALVES):
        got[t][n_col * TOUCH] = jnp.zeros((width, tile), jnp.bfloat16)
    load.wait()

    def compute(t):
        def body(i, acc):
            for u in range(UNROLL):
                p = i * UNROLL + u
                prod = lax.dot_general(
                    xbuf[t][scol[p]], tiles[perm[p]], (((1,), (1,)), ((), ())), preferred_element_type=jnp.float32
                )
                acc = jnp.where(cont[p] > 0, acc, 0.0) + prod
                run[p] = acc.astype(jnp.bfloat16)
            return acc

        lax.fori_loop(0, slots // UNROLL, body, jnp.zeros((width, tile), jnp.float32))

        def pack(s, carry):
            send[t, s] = run[ends[s]]
            return carry

        lax.fori_loop(0, n_col * TOUCH, pack, 0, unroll=4)
        for j in range(TOUCH):
            got[t][me_c * TOUCH + j] = run[ends[me_c * TOUCH + j]]

    def part_copy(t, d):
        peer = lax.rem(me_c + d, n_col)
        return pltpu.make_async_remote_copy(
            src_ref=send.at[t, pl.ds(peer * TOUCH, TOUCH)],
            dst_ref=got[t].at[pl.ds(me_c * TOUCH, TOUCH)],
            send_sem=send_sem.at[t, d], recv_sem=recv_sem.at[t, d],
            device_id=(me_r, peer), device_id_type=MESH,
        )

    def x_copy(t, d):
        mine = pl.ds(me_r * BPD, BPD)
        return pltpu.make_async_remote_copy(
            src_ref=xbuf[t + HALVES].at[mine], dst_ref=xbuf[t + HALVES].at[mine],
            send_sem=xsend_sem.at[t, d], recv_sem=xrecv_sem.at[t, d],
            device_id=(lax.rem(me_r + d, n_row), me_c), device_id_type=MESH,
        )

    def pos_copy(d):
        peer = lax.rem(me_c + d, n_col)
        return pltpu.make_async_remote_copy(
            src_ref=pos_ref.at[peer], dst_ref=posbuf.at[me_c],
            send_sem=pos_send.at[d], recv_sem=pos_recv.at[d],
            device_id=(me_r, peer), device_id_type=MESH,
        )

    def gather_wait(t):
        for d in range(1, n_row):
            x_copy(t, d).wait_recv()

    def reduce(t):
        k, h = divmod(t, HALVES)
        for d in range(1, n_col):
            part_copy(t, d).wait_recv()
        part = pl.ds(h * width, width)
        weight = coef[part, :]
        scale = weight
        for _ in range(k - 1):
            scale = scale * weight

        def block(b, carry):
            acc = got[t][pos_smem[0, 0, b]].astype(jnp.float32)
            for s in range(1, n_col):
                acc = acc + got[t][pos_smem[s, 0, b]].astype(jnp.float32)
            if k == 0:
                total[b, part, :] = acc
            else:
                total[b, part, :] = total[b, part, :] + scale * acc
            if k + 1 < TERMS:
                xbuf[t + HALVES][me_r * BPD + b] = acc.astype(jnp.bfloat16)
            return carry

        lax.fori_loop(0, BPD, block, 0)
        if k + 1 < TERMS:
            for d in range(1, n_row):
                x_copy(t, d).start()

    steps = TERMS * HALVES
    for t in range(steps + 1):
        if t < steps:
            if t >= HALVES:
                gather_wait(t - HALVES)
            compute(t)
            if t == 0:
                pl.semaphore_wait(barrier, n_col - 1 + n_row - 1)
                for d in range(1, n_col):
                    pos_copy(d).start()
            for d in range(1, n_col):
                part_copy(t, d).start()
            if t == 0:
                own = pltpu.make_async_copy(pos_ref.at[me_c], posbuf.at[me_c], local_sem)
                own.start()
                own.wait()
                for d in range(1, n_col):
                    pos_copy(d).wait_recv()
                spill = pltpu.make_async_copy(posbuf, pos_smem, local_sem)
                spill.start()
                spill.wait()
        if t >= 1:
            reduce(t - 1)

    for b in range(BPD):
        out_ref[pl.ds(b * tile, tile), :] = jnp.transpose(total[b])
    for d in range(1, n_col):
        pos_copy(d).wait_send()
        for t in range(steps):
            part_copy(t, d).wait_send()
    for d in range(1, n_row):
        for t in range(steps - HALVES):
            x_copy(t, d).wait_send()


def shards(tiles, tile_row, tile_col, tile_count, query_ids, damping):
    tile_block = tiles[0, 0]
    slots, tile, _ = tile_block.shape
    queries = query_ids.shape[0]
    n_row = lax.axis_size("row")
    n_col = lax.axis_size("col")
    me_col = lax.axis_index("col")
    perm, scol, cont, ends, pos = plan(tile_row[0, 0], tile_col[0, 0], tile_count[0, 0], n_col, me_col)
    width = queries // HALVES
    steps = TERMS * HALVES
    bf16 = jnp.bfloat16
    dma = pltpu.SemaphoreType.DMA
    smem = pl.BlockSpec(memory_space=pltpu.SMEM)
    vmem = pl.BlockSpec(memory_space=pltpu.VMEM)
    return pl.pallas_call(
        functools.partial(katz_kernel, n_row, n_col),
        out_shape=jax.ShapeDtypeStruct((BPD * tile, queries), jnp.float32),
        in_specs=[smem] * 4 + [vmem] * 3 + [pl.BlockSpec(memory_space=pl.ANY)],
        out_specs=vmem,
        scratch_shapes=[
            pltpu.VMEM((slots, tile, tile), bf16),
            pltpu.VMEM((slots, width, tile), bf16),
            pltpu.VMEM((steps, n_col * TOUCH, width, tile), bf16),
            [pltpu.VMEM((n_col * TOUCH + 1, width, tile), bf16)] * steps,
            [pltpu.VMEM((n_row * BPD, width, tile), bf16)] * steps,
            pltpu.VMEM((BPD, queries, tile), jnp.float32),
            pltpu.VMEM((queries, tile), jnp.float32),
            pltpu.VMEM((n_col, 1, 128), jnp.int32),
            pltpu.SMEM((n_col, 1, 128), jnp.int32),
            dma, dma((n_col,)), dma((n_col,)), dma,
            dma((steps, n_col)), dma((steps, n_col)),
            dma((steps - HALVES, n_row)), dma((steps - HALVES, n_row)),
        ],
        compiler_params=pltpu.CompilerParams(
            collective_id=0, has_side_effects=True, vmem_limit_bytes=60 * 1024 * 1024
        ),
    )(perm, scol, cont, ends, pos, query_ids.reshape(1, queries), damping.reshape(1, queries), tile_block)


def solution(mesh):
    in_specs = (
        P("row", "col", None, None, None),
        P("row", "col", None),
        P("row", "col", None),
        P("row", "col"),
        P(),
        P(),
    )
    out_specs = P(("row", "col"), None)
    return jax.shard_map(shards, mesh=mesh, in_specs=in_specs, out_specs=out_specs, check_vma=False)
```

time: 414 us -> 135 us (0.33)
  the two profiles are of different devices: /device:TPU:0 before, /device:TPU:25 now
where the time goes in v1:
time: 135 us; the launch traced here: 134 us
  Pallas kernels  127 us (94%)
  local copies, waits for them, and re-layouts  3.35 us (2%)
  other arithmetic  3.03 us (2%)
    pallas_call x1, Pallas kernels, shards(): pl.pallas_call(functools.partial(katz_kernel, n_row, n_col), out_shape=ja...  127 us

profile of v1, /device:TPU:25, one launch (start us, length us, event | category | flops | bytes accessed | tf_op | source)
XLA Modules:
  0.0 134.3 jit_solution(15661034249226826149)
XLA Ops:
  0.7 0.7 compare_select_fusion
  1.3 0.1 convert_reduce_fusion.1
  1.4 0.1 fusion.2
  1.5 0.1 and.29
  1.6 0.2 fusion.1
  1.8 0.2 convert_reduce_fusion
  2.0 1.4 %select_reduce_fusion = (s32[128]{0:T(128)}, s32[128]{0:T(128)}, s32[128]{0:T(128)}) fusion(s32[128]{0:T(128)S(1)} %convert_element_type.19, s32[128]{0:T(128)S(1)} %convert_reduce_fusion, s32[128]{0:T(128)} %bitcast.13), kind=kLoop, calls=%fused_computation | loop fusion | flops 114304 | bytes 3072 | tf_op jit(solution)/shard_map/reduce_sum | solution.py:30
  3.4 0.2 convert_reduce_fusion.2
  3.7 0.6 pad.4
  4.3 0.1 sub.7
  4.3 0.1 select_reduce_fusion.3
  4.5 0.1 copy.7
  4.6 0.6 reshape.60.ends
  5.2 127.2 %shard_map.64 = f32[1024,128]{1,0:T(8,128)} custom-call(s32[128]{0:T(128)} %get-tuple-element.7.perm, s32[128]{0:T(128)} %get-tuple-element.6.scol, s32[128]{0:T(128)} %get-tuple-element.5.cont, s32[32]{0:T(128)} %reshape.60.ends, s32[8,1,128]{2,1,0:T(1,128)} %bitcast.10, s32[1,128]{1,0:T(1,128)} %bitcast.11, f32[1,128]{1,0:T(1,128)} %bitcast.12, ...), custom_call_target="tpu_custom_call" | custom-call | tf_op jit(solution)/shard_map/pallas_call | solution.py:210
  132.4 1.9 %copy.10 = f32[1024,128]{1,0:T(8,128)} copy(f32[1024,128]{1,0:T(8,128)} %shard_map.64) | data formatting | bytes 1048576
  (4 shorter events, 0.0 us)

commit v2 on v1

--- a/solution.py
+++ b/solution.py
@@ -10,8 +10,8 @@
 BPD = 8
 TERMS = 4
 TOUCH = 4
-HALVES = 2
-UNROLL = 8
+GROUPS = 4
+UNROLL = 32
 MESH = pl.DeviceIdType.MESH
 
 
@@ -49,13 +49,13 @@
     pos_ref, qid_ref, damp_ref, tiles_hbm,
     out_ref,
     tiles, run, send, got, xbuf, total, coef, posbuf, pos_smem,
-    tile_sem, pos_send, pos_recv, local_sem, send_sem, recv_sem, xsend_sem, xrecv_sem,
+    tile_sem, pos_send, pos_recv, local_sem, send_sem, recv_sem, xsend_sem, xrecv_sem, xpass_sem,
 ):
     me_r = lax.axis_index("row")
     me_c = lax.axis_index("col")
     slots, tile, _ = tiles.shape
     queries = qid_ref.shape[1]
-    width = queries // HALVES
+    width = queries // GROUPS
 
     load = pltpu.make_async_copy(tiles_hbm, tiles, tile_sem)
     load.start()
@@ -72,12 +72,12 @@
     def first_x(j, carry):
         base = ((j // BPD * n_col + me_c) * BPD + lax.rem(j, BPD)) * tile
         hot = jnp.where(qid == base, 1.0, 0.0).astype(jnp.bfloat16)
-        for h in range(HALVES):
+        for h in range(GROUPS):
             xbuf[h][j] = hot[h * width:(h + 1) * width]
         return carry
 
     lax.fori_loop(0, n_row * BPD, first_x, 0)
-    for t in range(TERMS * HALVES):
+    for t in range(TERMS * GROUPS):
         got[t][n_col * TOUCH] = jnp.zeros((width, tile), jnp.bfloat16)
     load.wait()
 
@@ -107,16 +107,16 @@
         return pltpu.make_async_remote_copy(
             src_ref=send.at[t, pl.ds(peer * TOUCH, TOUCH)],
             dst_ref=got[t].at[pl.ds(me_c * TOUCH, TOUCH)],
-            send_sem=send_sem.at[t, d], recv_sem=recv_sem.at[t, d],
+            send_sem=send_sem.at[t], recv_sem=recv_sem.at[t],
             device_id=(me_r, peer), device_id_type=MESH,
         )
 
-    def x_copy(t, d):
-        mine = pl.ds(me_r * BPD, BPD)
-        return pltpu.make_async_remote_copy(
-            src_ref=xbuf[t + HALVES].at[mine], dst_ref=xbuf[t + HALVES].at[mine],
-            send_sem=xsend_sem.at[t, d], recv_sem=xrecv_sem.at[t, d],
-            device_id=(lax.rem(me_r + d, n_row), me_c), device_id_type=MESH,
+    def all_parts(t):
+        every = pl.ds(0, (n_col - 1) * TOUCH)
+        return pltpu.make_async_remote_copy(
+            src_ref=send.at[t, every], dst_ref=got[t].at[every],
+            send_sem=send_sem.at[t], recv_sem=recv_sem.at[t],
+            device_id=(me_r, lax.rem(me_c + 1, n_col)), device_id_type=MESH,
         )
 
     def pos_copy(d):
@@ -127,14 +127,56 @@
             device_id=(me_r, peer), device_id_type=MESH,
         )
 
-    def gather_wait(t):
-        for d in range(1, n_row):
-            x_copy(t, d).wait_recv()
+    is_end = (me_r == 0) | (me_r == n_row - 1)
+
+    def x_rows(t, first, count, peer, sems, where):
+        rows = pl.ds(first * BPD, count * BPD)
+        return pltpu.make_async_remote_copy(
+            src_ref=xbuf[t + GROUPS].at[rows], dst_ref=xbuf[t + GROUPS].at[rows],
+            send_sem=sems.at[t, where], recv_sem=(xpass_sem if where == n_row else xrecv_sem).at[t],
+            device_id=(peer, me_c), device_id_type=MESH,
+        )
+
+    def for_targets(t, act):
+        order = [(lax.rem(me_r + d, n_row), d) for d in (1, n_row - 1, *range(2, n_row - 1))]
+        for peer, d in order[:n_row - 1] if n_row > 2 else order[:1]:
+            far = jnp.abs(peer - me_r) > 1
+            skip = far & ((peer == 0) | (peer == n_row - 1))
+
+            @pl.when(jnp.logical_not(skip))
+            def _():
+                act(x_rows(t, me_r, 1, peer, xsend_sem, d))
+
+    def for_passes(t, act):
+        if n_row > 2:
+            @pl.when(me_r == 1)
+            def _():
+                act(x_rows(t, 2, n_row - 2, 0, xsend_sem, n_row))
+
+            @pl.when(me_r == n_row - 2)
+            def _():
+                act(x_rows(t, 0, n_row - 2, n_row - 1, xsend_sem, n_row))
+
+    def x_pass(t):
+        @pl.when(is_end)
+        def _():
+            x_rows(t, 0, 1, lax.rem(me_r + 1, n_row), xsend_sem, 0).wait_recv()
+
+        @pl.when(jnp.logical_not(is_end))
+        def _():
+            x_rows(t, 0, n_row - 1, lax.rem(me_r + 1, n_row), xsend_sem, 0).wait_recv()
+
+        for_passes(t, lambda copy: copy.start())
+
+    def x_ready(t):
+        if n_row > 2:
+            @pl.when(is_end)
+            def _():
+                x_rows(t, 0, n_row - 2, lax.rem(me_r + 1, n_row), xsend_sem, n_row).wait_recv()
 
     def reduce(t):
-        k, h = divmod(t, HALVES)
-        for d in range(1, n_col):
-            part_copy(t, d).wait_recv()
+        k, h = divmod(t, GROUPS)
+        all_parts(t).wait_recv()
         part = pl.ds(h * width, width)
         weight = coef[part, :]
         scale = weight
@@ -150,19 +192,19 @@
             else:
                 total[b, part, :] = total[b, part, :] + scale * acc
             if k + 1 < TERMS:
-                xbuf[t + HALVES][me_r * BPD + b] = acc.astype(jnp.bfloat16)
+                xbuf[t + GROUPS][me_r * BPD + b] = acc.astype(jnp.bfloat16)
             return carry
 
         lax.fori_loop(0, BPD, block, 0)
         if k + 1 < TERMS:
-            for d in range(1, n_row):
-                x_copy(t, d).start()
-
-    steps = TERMS * HALVES
+            for_targets(t, lambda copy: copy.start())
+
+    steps = TERMS * GROUPS
+    moves = steps - GROUPS
     for t in range(steps + 1):
         if t < steps:
-            if t >= HALVES:
-                gather_wait(t - HALVES)
+            if t >= GROUPS:
+                x_ready(t - GROUPS)
             compute(t)
             if t == 0:
                 pl.semaphore_wait(barrier, n_col - 1 + n_row - 1)
@@ -181,16 +223,18 @@
                 spill.wait()
         if t >= 1:
             reduce(t - 1)
+        if 2 <= t < moves + 2:
+            x_pass(t - 2)
 
     for b in range(BPD):
         out_ref[pl.ds(b * tile, tile), :] = jnp.transpose(total[b])
     for d in range(1, n_col):
         pos_copy(d).wait_send()
-        for t in range(steps):
-            part_copy(t, d).wait_send()
-    for d in range(1, n_row):
-        for t in range(steps - HALVES):
-            x_copy(t, d).wait_send()
+    for t in range(steps):
+        all_parts(t).wait_send()
+    for t in range(moves):
+        for_targets(t, lambda copy: copy.wait_send())
+        for_passes(t, lambda copy: copy.wait_send())
 
 
 def shards(tiles, tile_row, tile_col, tile_count, query_ids, damping):
@@ -201,8 +245,9 @@
     n_col = lax.axis_size("col")
     me_col = lax.axis_index("col")
     perm, scol, cont, ends, pos = plan(tile_row[0, 0], tile_col[0, 0], tile_count[0, 0], n_col, me_col)
-    width = queries // HALVES
-    steps = TERMS * HALVES
+    width = queries // GROUPS
+    steps = TERMS * GROUPS
+    moves = steps - GROUPS
     bf16 = jnp.bfloat16
     dma = pltpu.SemaphoreType.DMA
     smem = pl.BlockSpec(memory_space=pltpu.SMEM)
@@ -223,8 +268,8 @@
             pltpu.VMEM((n_col, 1, 128), jnp.int32),
             pltpu.SMEM((n_col, 1, 128), jnp.int32),
             dma, dma((n_col,)), dma((n_col,)), dma,
-            dma((steps, n_col)), dma((steps, n_col)),
-            dma((steps - HALVES, n_row)), dma((steps - HALVES, n_row)),
+            dma((steps,)), dma((steps,)),
+            dma((moves, n_row + 1)), dma((moves,)), dma((moves,)),
         ],
         compiler_params=pltpu.CompilerParams(
             collective_id=0, has_side_effects=True, vmem_limit_bytes=60 * 1024 * 1024

time: 135 us -> 90.1 us (0.67)
  the two profiles are of different devices: /device:TPU:25 before, /device:TPU:0 now
where the time goes in v2:
time: 90.1 us; the launch traced here: 89.8 us
  Pallas kernels  82.7 us (92%)
  local copies, waits for them, and re-layouts  3.35 us (4%)
  other arithmetic  3.03 us (3%)
    pallas_call x1, Pallas kernels, shards(): pl.pallas_call(functools.partial(katz_kernel, n_row, n_col), out_shape=ja...  82.7 us
    unnamed x1, local copies, waits for them, and re-layouts  1.87 us

profile of v2, /device:TPU:0, one launch (start us, length us, event | category | flops | bytes accessed | tf_op | source)
XLA Modules:
  0.0 89.8 jit_solution(4627822811485722682)
XLA Ops:
  0.7 0.7 compare_select_fusion
  1.3 0.1 convert_reduce_fusion.1
  1.4 0.1 fusion.2
  1.5 0.1 and.29
  1.6 0.2 fusion.1
  1.8 0.2 convert_reduce_fusion
  2.0 1.4 %select_reduce_fusion = (s32[128]{0:T(128)}, s32[128]{0:T(128)}, s32[128]{0:T(128)}) fusion(s32[128]{0:T(128)S(1)} %convert_element_type.19, s32[128]{0:T(128)S(1)} %convert_reduce_fusion, s32[128]{0:T(128)} %bitcast.13), kind=kLoop, calls=%fused_computation | loop fusion | flops 114304 | bytes 3072 | tf_op jit(solution)/shard_map/reduce_sum | solution.py:30
  3.4 0.2 convert_reduce_fusion.2
  3.7 0.6 pad.4
  4.3 0.1 sub.7
  4.3 0.1 select_reduce_fusion.3
  4.5 0.1 copy.7
  4.6 0.6 reshape.60.ends
  5.2 82.7 %shard_map.64 = f32[1024,128]{1,0:T(8,128)} custom-call(s32[128]{0:T(128)} %get-tuple-element.7.perm, s32[128]{0:T(128)} %get-tuple-element.6.scol, s32[128]{0:T(128)} %get-tuple-element.5.cont, s32[32]{0:T(128)} %reshape.60.ends, s32[8,1,128]{2,1,0:T(1,128)} %bitcast.10, s32[1,128]{1,0:T(1,128)} %bitcast.11, f32[1,128]{1,0:T(1,128)} %bitcast.12, ...), custom_call_target="tpu_custom_call" | custom-call | tf_op jit(solution)/shard_map/pallas_call | solution.py:255
  87.9 1.9 %copy.10 = f32[1024,128]{1,0:T(8,128)} copy(f32[1024,128]{1,0:T(8,128)} %shard_map.64) | data formatting | bytes 1048576
  (4 shorter events, 0.0 us)

commit v3 on v2

--- a/solution.py
+++ b/solution.py
@@ -11,7 +11,7 @@
 TERMS = 4
 TOUCH = 4
 GROUPS = 4
-UNROLL = 32
+UNROLL = 64
 MESH = pl.DeviceIdType.MESH
 
 
@@ -48,7 +48,7 @@
     perm, scol, cont, ends,
     pos_ref, qid_ref, damp_ref, tiles_hbm,
     out_ref,
-    tiles, run, send, got, xbuf, total, coef, posbuf, pos_smem,
+    tiles, flip, run, send, got, xbuf, total, coef, posbuf, pos_smem,
     tile_sem, pos_send, pos_recv, local_sem, send_sem, recv_sem, xsend_sem, xrecv_sem, xpass_sem,
 ):
     me_r = lax.axis_index("row")
@@ -83,13 +83,17 @@
 
     def compute(t):
         def body(i, acc):
-            for u in range(UNROLL):
+            for u in range(0, UNROLL, 2):
                 p = i * UNROLL + u
-                prod = lax.dot_general(
-                    xbuf[t][scol[p]], tiles[perm[p]], (((1,), (1,)), ((), ())), preferred_element_type=jnp.float32
-                )
-                acc = jnp.where(cont[p] > 0, acc, 0.0) + prod
+                if t == 0:
+                    flip[p // 2, :, :tile] = jnp.transpose(tiles[perm[p]])
+                    flip[p // 2, :, tile:] = jnp.transpose(tiles[perm[p + 1]])
+                both = jnp.concatenate([xbuf[t][scol[p]], xbuf[t][scol[p + 1]]], axis=0)
+                prod = jnp.dot(both, flip[p // 2], preferred_element_type=jnp.float32)
+                acc = jnp.where(cont[p] > 0, acc, 0.0) + prod[:width, :tile]
                 run[p] = acc.astype(jnp.bfloat16)
+                acc = jnp.where(cont[p + 1] > 0, acc, 0.0) + prod[width:, tile:]
+                run[p + 1] = acc.astype(jnp.bfloat16)
             return acc
 
         lax.fori_loop(0, slots // UNROLL, body, jnp.zeros((width, tile), jnp.float32))
@@ -98,7 +102,7 @@
             send[t, s] = run[ends[s]]
             return carry
 
-        lax.fori_loop(0, n_col * TOUCH, pack, 0, unroll=4)
+        lax.fori_loop(0, n_col * TOUCH, pack, 0, unroll=n_col * TOUCH)
         for j in range(TOUCH):
             got[t][me_c * TOUCH + j] = run[ends[me_c * TOUCH + j]]
 
@@ -195,7 +199,7 @@
                 xbuf[t + GROUPS][me_r * BPD + b] = acc.astype(jnp.bfloat16)
             return carry
 
-        lax.fori_loop(0, BPD, block, 0)
+        lax.fori_loop(0, BPD, block, 0, unroll=BPD)
         if k + 1 < TERMS:
             for_targets(t, lambda copy: copy.start())
 
@@ -212,7 +216,7 @@
                     pos_copy(d).start()
             for d in range(1, n_col):
                 part_copy(t, d).start()
-            if t == 0:
+            if t == 1:
                 own = pltpu.make_async_copy(pos_ref.at[me_c], posbuf.at[me_c], local_sem)
                 own.start()
                 own.wait()
@@ -259,6 +263,7 @@
         out_specs=vmem,
         scratch_shapes=[
             pltpu.VMEM((slots, tile, tile), bf16),
+            pltpu.VMEM((slots // 2, tile, 2 * tile), bf16),
             pltpu.VMEM((slots, width, tile), bf16),
             pltpu.VMEM((steps, n_col * TOUCH, width, tile), bf16),
             [pltpu.VMEM((n_col * TOUCH + 1, width, tile), bf16)] * steps,

time: 90.1 us -> 84 us (0.932)
  Pallas kernels: 82.7 us -> 76.7 us
    pallas_call x1, Pallas kernels: 82.7 us -> 76.7 us  [shards(): pl.pallas_call(functools.partial(katz_kernel, n_row, n_col), out_shape=ja...]
where the time goes in v3:
time: 84 us; the launch traced here: 83.8 us
  Pallas kernels  76.7 us (91%)
  local copies, waits for them, and re-layouts  3.35 us (4%)
  other arithmetic  3.03 us (4%)
    pallas_call x1, Pallas kernels, shards(): pl.pallas_call(functools.partial(katz_kernel, n_row, n_col), out_shape=ja...  76.7 us
    unnamed x1, local copies, waits for them, and re-layouts  1.87 us

profile of v3, /device:TPU:0, one launch (start us, length us, event | category | flops | bytes accessed | tf_op | source)
XLA Modules:
  0.0 83.8 jit_solution(17302500833217831440)
XLA Ops:
  0.7 0.7 compare_select_fusion
  1.3 0.1 convert_reduce_fusion.1
  1.4 0.1 fusion.2
  1.5 0.1 and.29
  1.6 0.2 fusion.1
  1.8 0.2 convert_reduce_fusion
  2.0 1.4 %select_reduce_fusion = (s32[128]{0:T(128)}, s32[128]{0:T(128)}, s32[128]{0:T(128)}) fusion(s32[128]{0:T(128)S(1)} %convert_element_type.19, s32[128]{0:T(128)S(1)} %convert_reduce_fusion, s32[128]{0:T(128)} %bitcast.13), kind=kLoop, calls=%fused_computation | loop fusion | flops 114304 | bytes 3072 | tf_op jit(solution)/shard_map/reduce_sum | solution.py:30
  3.4 0.2 convert_reduce_fusion.2
  3.7 0.6 pad.4
  4.3 0.1 sub.7
  4.3 0.1 select_reduce_fusion.3
  4.5 0.1 copy.7
  4.6 0.6 reshape.60.ends
  5.2 76.7 %shard_map.64 = f32[1024,128]{1,0:T(8,128)} custom-call(s32[128]{0:T(128)} %get-tuple-element.7.perm, s32[128]{0:T(128)} %get-tuple-element.6.scol, s32[128]{0:T(128)} %get-tuple-element.5.cont, s32[32]{0:T(128)} %reshape.60.ends, s32[8,1,128]{2,1,0:T(1,128)} %bitcast.10, s32[1,128]{1,0:T(1,128)} %bitcast.11, f32[1,128]{1,0:T(1,128)} %bitcast.12, ...), custom_call_target="tpu_custom_call" | custom-call | tf_op jit(solution)/shard_map/pallas_call | solution.py:259
  81.9 1.9 %copy.10 = f32[1024,128]{1,0:T(8,128)} copy(f32[1024,128]{1,0:T(8,128)} %shard_map.64) | data formatting | bytes 1048576
  (4 shorter events, 0.0 us)
